TPU v7x, 512 devices: a whole 4x8x8 slice. The times are simulated.
512 devices in a mesh: tm: 8 (over x, core), src: 64 (over y, z).
Axes of the slice: x: 4, y: 8, z: 8, core: 2. Of those that a mesh axis runs over, the one named last changes fastest.
Arguments:
- design: float32 [16, 8388608], P(None, ('tm', 'src')), may hold values from -2 to 2
- unit_index: int32 [8388608], P(('tm', 'src')), may hold values from 0 to 4095, as said below
- residual: float32 [8388608], P(('tm', 'src')), may hold values from -6 to 6
- weight: float32 [8388608], P(('tm', 'src')), may hold values from 0.25 to 4
- obs_count: int32 [512], P(('tm', 'src')), may hold values from 1 to 16384, as said below
- damping: float32 [4096], P(('tm', 'src')), may hold values from 1 to 10
Outputs:
- solution: float32 [16, 4096], P(None, ('tm', 'src'))
- misfit: float32 [], replicated
Inputs may be any that keep to these rules, and one draw needn't show every extreme that they name: `unit_index`: an observation on a device of tm index g names a unit in [g * 512, (g + 1) * 512). `obs_count`: some device has all 16384 slots live.
All inputs are finite; a program needn't handle non-finite values.
Results may differ from a plain program's by a relative error of at most 0.0003.
Values sent between devices are 32-bit elements; how exact they have to be, the bound alone decides.
A program may use at most 64 MiB of HBM per device.

v0:
```python
import jax
import jax.numpy as jnp
from jax import lax
from jax.sharding import Mesh
from jax.sharding import PartitionSpec as P

SRC = ("src_0", "src_1")
TM = ("tm_0", "tm_1")
TM_SRC = ("tm_0", "tm_1", "src_0", "src_1")


def in_blocks(x, dim, devices):
    dims = x.shape
    pieces = x.reshape(*dims[:dim], devices, dims[dim] // devices, *dims[dim + 1 :])
    return jnp.moveaxis(pieces, dim, 0)


def summed_on_arrival(x, axis, dim):
    pieces = in_blocks(x, dim, lax.axis_size(axis))
    arrived = lax.all_to_all(pieces, axis, split_axis=0, concat_axis=0, tiled=True)
    return arrived.sum(axis=0)


def by_axis(x, axes):
    for axis in axes:
        x = lax.psum(x, axis)
    return x


def make_reader(stacked):

    def reader(row, column):
        return stacked[row * 16 + column]

    return reader


def block_solve(reader, rhs, damping):
    lower = {}
    for j in range(16):
        running = reader(j, j) + damping
        for k in range(j):
            running = running - lower[j, k] * lower[j, k]
        diag_term = jnp.sqrt(running)
        lower[j, j] = diag_term
        for i in range(j + 1, 16):
            running = reader(i, j)
            for k in range(j):
                running = running - lower[i, k] * lower[j, k]
            lower[i, j] = running / diag_term
    forward = []
    for i in range(16):
        running = rhs[i]
        for k in range(i):
            running = running - lower[i, k] * forward[k]
        forward.append(running / lower[i, i])
    backward = [None] * 16
    for i in range(15, -1, -1):
        running = forward[i]
        for k in range(i + 1, 16):
            running = running - lower[k, i] * backward[k]
        backward[i] = running / lower[i, i]
    return jnp.stack(backward)


def quadratic_terms(reader, rhs, solution_own):
    quadratic = jnp.zeros((), jnp.float32)
    for i in range(16):
        applied = jnp.zeros_like(solution_own[0])
        for j in range(16):
            applied = applied + reader(max(i, j), min(i, j)) * solution_own[j]
        quadratic = quadratic + jnp.sum(solution_own[i] * applied)
    return quadratic - 2.0 * jnp.sum(solution_own * rhs)


def on_device(design, unit_index, residual, weight, obs_count, damping):
    n_source = lax.axis_size(SRC)
    own_units = damping.shape[0]
    units_group = own_units * n_source
    slots = design.shape[1]
    local_unit = unit_index - lax.axis_index(TM) * units_group
    weights_on = jnp.where(
        jnp.arange(slots, dtype=jnp.int32) < obs_count[0], weight, jnp.zeros_like(weight)
    )
    block_rows = 1024
    turns = slots // block_rows
    pair_count = 256

    def pair_rows(rows):
        return (rows[:, None, :] * rows[None, :, :]).reshape(256, rows.shape[1])

    unit_range = jnp.arange(units_group, dtype=jnp.int32)

    def accumulate(step, partial_value):
        begin = step * block_rows
        rows = lax.dynamic_slice_in_dim(design, begin, block_rows, 1)
        units_of = lax.dynamic_slice_in_dim(local_unit, begin, block_rows, 0)
        resid = lax.dynamic_slice_in_dim(residual, begin, block_rows, 0)
        weights_blk = lax.dynamic_slice_in_dim(weights_on, begin, block_rows, 0)
        stacked = jnp.concatenate(
            [pair_rows(rows) * weights_blk, rows * (weights_blk * resid)], axis=0
        )
        one_hot = (units_of[:, None] == unit_range[None, :]).astype(jnp.float32)
        return partial_value + jnp.dot(
            stacked, one_hot, precision=lax.Precision.HIGHEST, preferred_element_type=jnp.float32
        )

    start = jnp.zeros((pair_count + 16, units_group), jnp.float32)
    partial_value = lax.fori_loop(0, turns, accumulate, start)
    own_part = summed_on_arrival(partial_value, SRC, 1)
    solution_own = block_solve(make_reader(own_part), own_part[pair_count:], damping)
    unit_terms = quadratic_terms(make_reader(own_part), own_part[pair_count:], solution_own)
    before = jnp.sum(weights_on * residual * residual)
    chi_total, weight_total = (
        by_axis(before + unit_terms, TM_SRC),
        by_axis(jnp.sum(weights_on), TM_SRC),
    )
    return (solution_own, chi_total / weight_total)


def solution(mesh):
    torus = Mesh(mesh.devices.reshape(4, 2, 8, 8), ("tm_0", "tm_1", "src_0", "src_1"))
    return jax.shard_map(
        on_device,
        mesh=torus,
        in_specs=(P(None, TM_SRC), P(TM_SRC), P(TM_SRC), P(TM_SRC), P(TM_SRC), P(TM_SRC)),
        out_specs=(P(None, TM_SRC), P()),
        check_vma=False,
    )
```

profile of v0, /device:TPU:8, one launch (start us, length us, event | category | flops | bytes accessed | tf_op | source)
XLA Modules:
  0.0 174.0 jit_solution(1141471634184720458)
XLA Ops:
  1.3 0.8 broadcast_subtract_fusion
  2.1 1.6 fusion.12
  3.7 52.6 %while.14 = (s32[]{:T(128)}, f32[272,512]{1,0:T(8,128)S(1)}, f32[16,16384]{1,0:T(8,128)}, f32[16384]{0:T(1024)S(1)}, f32[16384]{0:T(1024)}, /*index=5*/s32[16384...) while((s32[]{:T(128)}, f32[272,512]{1,0:T(8,128)S(1)}, f32[16,16384]{1,0:T(8,128)}, ...), condition=%wide.region_1.2_spmd.clone, body=%wide.region_0.1_spmd.clone.sunk | while | flops 1712899072 | bytes 5673129 | solution.py:109
  4.4 0.8 broadcast_multiply_fusion.4
  5.5 1.4 fusion.17
  7.7 0.8 broadcast_multiply_fusion.4
  8.8 1.4 fusion.17
  10.3 0.7 dynamic-slice_multiply_fusion.2
  11.0 0.8 broadcast_multiply_fusion.4
  12.1 1.4 fusion.17
  14.3 0.8 broadcast_multiply_fusion.4
  15.4 1.4 fusion.17
  16.9 0.7 dynamic-slice_multiply_fusion.2
  17.6 0.8 broadcast_multiply_fusion.4
  18.7 1.4 fusion.17
  20.1 0.7 dynamic-slice_multiply_fusion.2
  20.8 0.8 broadcast_multiply_fusion.4
  22.0 1.4 fusion.17
  23.4 0.7 dynamic-slice_multiply_fusion.2
  24.1 0.8 broadcast_multiply_fusion.4
  25.3 1.4 fusion.17
  26.7 0.7 dynamic-slice_multiply_fusion.2
  27.4 0.8 broadcast_multiply_fusion.4
  28.6 1.4 fusion.17
  30.0 0.7 dynamic-slice_multiply_fusion.2
  30.7 0.8 broadcast_multiply_fusion.4
  31.8 1.4 fusion.17
  34.0 0.8 broadcast_multiply_fusion.4
  35.1 1.4 fusion.17
  37.3 0.8 broadcast_multiply_fusion.4
  38.4 1.4 fusion.17
  40.6 0.8 broadcast_multiply_fusion.4
  41.7 1.4 fusion.17
  43.9 0.8 broadcast_multiply_fusion.4
  45.0 1.4 fusion.17
  47.1 0.8 broadcast_multiply_fusion.4
  48.3 1.4 fusion.17
  50.4 0.8 broadcast_multiply_fusion.4
  51.6 1.4 fusion.17
  53.7 0.8 broadcast_multiply_fusion.4
  54.9 1.4 fusion.17
  56.6 40.2 %all_to_all.5 = f32[64,272,8]{1,2,0:T(8,128)S(1)} all-to-all(f32[64,272,8]{1,2,0:T(8,128)S(1)} %bitcast.25), channel_id=1, replica_groups=mesh['tm_0'=4,'tm_1'=2,'src_0'=8,'src_1'=8] {'src_0','src_1'}, dimensions={0} | all-to-all | bytes 1114112 | tf_op jit(solution)/shard_map/all_to_all | solution.py:20
  101.6 0.9 multiply_reduce_fusion
  105.8 0.7 multiply_reduce_fusion.6
  125.5 11.0 %all-reduce.2 = (f32[]{:T(128)}, f32[]{:T(128)}) all-reduce(f32[]{:T(128)S(6)} %add.1140, f32[]{:T(128)} %get-tuple-element.154), channel_id=1, replica_groups=mesh['tm_0'=4,'tm_1'=2,'src_0'=8,'src_1'=8] {'tm_0'}, use_global_device_ids=true, to_apply=%region_21.22 | all-reduce | flops 2 | bytes 16 | tf_op jit(solution)/shard_map/psum | solution.py:26
  136.5 3.2 %all-reduce.3 = (f32[]{:T(128)}, f32[]{:T(128)}) all-reduce(f32[]{:T(128)} %get-tuple-element.324, f32[]{:T(128)} %get-tuple-element.325), channel_id=1, replica_groups=mesh['tm_0'=4,'tm_1'=2,'src_0'=8,'src_1'=8] {'tm_1'}, use_global_device_ids=true, to_apply=%region_22.23 | all-reduce | flops 2 | bytes 16 | tf_op jit(solution)/shard_map/psum | solution.py:26
  139.7 16.0 %all-reduce.1 = (f32[]{:T(128)}, f32[]{:T(128)}) all-reduce(f32[]{:T(128)} %get-tuple-element.326, f32[]{:T(128)} %get-tuple-element.327), channel_id=1, replica_groups=mesh['tm_0'=4,'tm_1'=2,'src_0'=8,'src_1'=8] {'src_0'}, use_global_device_ids=true, to_apply=%region_23.24 | all-reduce | flops 2 | bytes 16 | tf_op jit(solution)/shard_map/psum | solution.py:26
  155.7 15.8 %all-reduce = (f32[]{:T(128)}, f32[]{:T(128)}) all-reduce(f32[]{:T(128)} %get-tuple-element.322, f32[]{:T(128)} %get-tuple-element.323), channel_id=1, replica_groups=mesh['tm_0'=4,'tm_1'=2,'src_0'=8,'src_1'=8] {'src_1'}, use_global_device_ids=true, to_apply=%region_24.25 | all-reduce | flops 2 | bytes 16 | tf_op jit(solution)/shard_map/psum | solution.py:26
  (107 shorter events, 27.2 us)
Async XLA Ops:
  96.8 4.2 %copy-start.1 = (f32[8]{0:T(128)S(1)}, f32[8]{0:T(128)}, u32[]{:S(2)}) copy-start(f32[8]{0:T(128)} %param.13) | copy-start | bytes 100
  113.8 59.1 %copy-start = (f32[16,8]{0,1:T(8,128)}, f32[16,8]{0,1:T(8,128)S(1)}, u32[]{:S(2)}) copy-start(f32[16,8]{0,1:T(8,128)S(1)} %stack.67) | copy-start | bytes 1540
where the time goes:
time: 176 us; the launch traced here: 174 us
  blocking collectives  86.2 us (49%)
  other arithmetic  43.1 us (24%)
  matrix products  22.9 us (13%)
  between operations  15 us (9%)
  local copies, waits for them, and re-layouts  5.88 us (3%)
    psum x4, blocking collectives, by_axis(): x = lax.psum(x, axis)  46 us
    all_to_all x1, blocking collectives, summed_on_arrival(): lax.all_to_all(pieces, axis, split_axis=0, concat_axis=0, tiled=True)  40.2 us
    dot_general x16, matrix products, accumulate(): jnp.dot(stacked, one_hot, precision=lax.Precision.HIGHEST, preferred_elem...  22.9 us
    mul x16, other arithmetic, accumulate(): rows * (weights_blk * resid)  13.6 us
    mul x16, other arithmetic, accumulate(): weights_blk * resid  11.1 us
    reduce_sum x16, other arithmetic, quadratic_terms(): quadratic = quadratic + jnp.sum(solution_own[i] * applied)  10.8 us
    slice x7, local copies, waits for them, and re-layouts, block_solve(): running = rhs[i]  3.55 us

commit v1 on v0

--- a/solution.py
+++ b/solution.py
@@ -23,7 +23,7 @@
 
 def by_axis(x, axes):
     for axis in axes:
-        x = lax.psum(x, axis)
+        x = jnp.sum(lax.all_gather(x, axis), axis=0)
     return x
 
 

time: 176 us -> 193 us (1.097)
  blocking collectives: 86.2 us -> 43.3 us
  waiting for transfers between devices: 0 us -> 21.3 us
  starting transfers between devices: 0 us -> 16.6 us
  local copies, waits for them, and re-layouts: 5.88 us -> 22.4 us
  other arithmetic: 43.1 us -> 47.9 us
    psum x4 -> x0, blocking collectives: 46 us -> none  [by_axis(): x = lax.psum(x, axis)]
    unnamed x0 -> x4, blocking collectives: none -> 43.3 us
    all_to_all x1 -> x0, blocking collectives: 40.2 us -> none  [summed_on_arrival(): lax.all_to_all(pieces, axis, split_axis=0, concat_axis=0, tiled=True)]
    all_to_all x0 -> x1, waiting for transfers between devices: none -> 21.3 us  [summed_on_arrival(): lax.all_to_all(pieces, axis, split_axis=0, concat_axis=0, tiled=True)]
    all_to_all x0 -> x1, starting transfers between devices: none -> 16.6 us  [summed_on_arrival(): lax.all_to_all(pieces, axis, split_axis=0, concat_axis=0, tiled=True)]
    unnamed x4 -> x24, local copies, waits for them, and re-layouts: 0.01 us -> 15.6 us
    reduce_sum x0 -> x8, other arithmetic: none -> 4.87 us  [by_axis(): x = jnp.sum(lax.all_gather(x, axis), axis=0)]
  transfers between devices with their start and end apart: 0 -> 1, of which waited for: 0 -> 1; matrix products, arithmetic and copies ran while one was open for 0% -> 1% of each run, Pallas kernels for 0% -> 0%
where the time goes in v1:
time: 193 us; the launch traced here: 191 us
  other arithmetic  47.9 us (25%)
  blocking collectives  43.3 us (22%)
  matrix products  22.9 us (12%)
  local copies, waits for them, and re-layouts  22.4 us (12%)
  waiting for transfers between devices  21.3 us (11%)
  starting transfers between devices  16.6 us (9%)
  between operations  15.1 us (8%)
    unnamed x4, blocking collectives  43.3 us
    dot_general x16, matrix products, accumulate(): jnp.dot(stacked, one_hot, precision=lax.Precision.HIGHEST, preferred_elem...  22.9 us
    all_to_all x1, waiting for transfers between devices, summed_on_arrival(): lax.all_to_all(pieces, axis, split_axis=0, concat_axis=0, tiled=True)  21.3 us
    all_to_all x1, starting transfers between devices, summed_on_arrival(): lax.all_to_all(pieces, axis, split_axis=0, concat_axis=0, tiled=True)  16.6 us
    unnamed x24, local copies, waits for them, and re-layouts  15.6 us
    mul x16, other arithmetic, accumulate(): rows * (weights_blk * resid)  13.6 us
    mul x16, other arithmetic, accumulate(): weights_blk * resid  11.1 us
    reduce_sum x16, other arithmetic, quadratic_terms(): quadratic = quadratic + jnp.sum(solution_own[i] * applied)  10.7 us
  transfers between devices with their start and end apart: 1, of which 1 were waited for; matrix products, arithmetic and copies ran while one was open for 1% of the time, Pallas kernels for 0%

profile of v1, /device:TPU:8, one launch (start us, length us, event | category | flops | bytes accessed | tf_op | source)
XLA Modules:
  0.0 190.5 jit_solution(13602585734821873553)
XLA Ops:
  2.1 1.6 fusion.12
  3.7 52.6 %while.14 = (s32[]{:T(128)}, f32[272,512]{1,0:T(8,128)S(1)}, f32[16,16384]{1,0:T(8,128)}, f32[16384]{0:T(1024)S(1)}, f32[16384]{0:T(1024)}, /*index=5*/s32[16384...) while((s32[]{:T(128)}, f32[272,512]{1,0:T(8,128)S(1)}, f32[16,16384]{1,0:T(8,128)}, ...), condition=%wide.region_1.2_spmd.clone, body=%wide.region_0.1_spmd.clone.sunk | while | flops 1712899072 | bytes 5673129 | solution.py:109
  4.4 0.8 broadcast_multiply_fusion.4
  5.5 1.4 fusion.17
  7.7 0.8 broadcast_multiply_fusion.4
  8.8 1.4 fusion.17
  11.0 0.8 broadcast_multiply_fusion.4
  12.1 1.4 fusion.17
  14.3 0.8 broadcast_multiply_fusion.4
  15.4 1.4 fusion.17
  17.5 0.8 broadcast_multiply_fusion.4
  18.7 1.4 fusion.17
  22.0 1.4 fusion.17
  25.3 1.4 fusion.17
  27.4 0.8 broadcast_multiply_fusion.4
  28.5 1.4 fusion.17
  31.8 1.4 fusion.17
  34.0 0.8 broadcast_multiply_fusion.4
  35.1 1.4 fusion.17
  37.3 0.8 broadcast_multiply_fusion.4
  38.4 1.4 fusion.17
  40.6 0.8 broadcast_multiply_fusion.4
  41.7 1.4 fusion.17
  45.0 1.4 fusion.17
  47.1 0.8 broadcast_multiply_fusion.4
  48.3 1.4 fusion.17
  51.6 1.4 fusion.17
  53.7 0.8 broadcast_multiply_fusion.4
  54.8 1.4 fusion.17
  56.3 1.1 copy.28
  57.4 16.6 %all-to-all-start = ((f32[64,272,8]{1,2,0:T(8,128)}), f32[64,272,8]{1,2,0:T(8,128)S(1)}, u32[]{:S(2)}, u32[]{:S(2)}) async-start(f32[64,272,8]{1,2,0:T(8,128)} %bitcast.2), calls=%async_computation | async-start | bytes 1572864 | tf_op jit(solution)/shard_map/all_to_all | solution.py:20
  74.0 1.2 dynamic-slice
  75.3 1.3 dynamic-update-slice.4
  76.6 21.3 %all-to-all-done = f32[64,272,8]{1,2,0:T(8,128)S(1)} async-done(((f32[64,272,8]{1,2,0:T(8,128)}), f32[64,272,8]{1,2,0:T(8,128)S(1)}, u32[]{:S(2)}, u32[]{:S(2)}) %all-to-all-start) | async-done | bytes 557088 | tf_op jit(solution)/shard_map/all_to_all | solution.py:20
  102.7 0.9 multiply_reduce_fusion
  127.3 1.3 dynamic-slice.1
  128.7 10.5 %all-reduce.10 = (f32[4]{0:T(128)S(1)}, f32[4]{0:T(128)S(1)}) all-reduce(f32[4]{0:T(128)S(1)} %dynamic-update-slice, f32[4]{0:T(128)S(1)} %dynamic-update-slice.4), channel_id=1, replica_groups=mesh['tm_0'=4,'tm_1'=2,'src_0'=8,'src_1'=8] {'tm_0'}, use_global_device_ids=true, to_apply=%add | all-reduce | flops 8 | bytes 64
  140.3 1.4 dynamic-update-slice.5
  141.7 1.4 dynamic-update-slice.1
  143.1 1.3 dynamic-slice.2
  144.5 2.4 %all-reduce.11 = (f32[2]{0:T(128)S(1)}, f32[2]{0:T(128)S(1)}) all-reduce(f32[2]{0:T(128)S(1)} %dynamic-update-slice.1, f32[2]{0:T(128)S(1)} %dynamic-update-slice.5), channel_id=1, replica_groups=mesh['tm_0'=4,'tm_1'=2,'src_0'=8,'src_1'=8] {'tm_1'}, use_global_device_ids=true, to_apply=%add.1 | all-reduce | flops 4 | bytes 32
  148.1 1.4 dynamic-update-slice.6
  149.5 1.4 dynamic-update-slice.2
  150.9 1.3 dynamic-slice.3
  152.3 15.4 %all-reduce.9 = (f32[8]{0:T(128)S(1)}, f32[8]{0:T(128)S(1)}) all-reduce(f32[8]{0:T(128)S(1)} %dynamic-update-slice.2, f32[8]{0:T(128)S(1)} %dynamic-update-slice.6), channel_id=1, replica_groups=mesh['tm_0'=4,'tm_1'=2,'src_0'=8,'src_1'=8] {'src_0'}, use_global_device_ids=true, to_apply=%add.2 | all-reduce | flops 16 | bytes 128
  168.9 1.4 dynamic-update-slice.7
  170.2 1.4 dynamic-update-slice.3
  171.7 15.1 %all-reduce.8 = (f32[8]{0:T(128)S(1)}, f32[8]{0:T(128)S(1)}) all-reduce(f32[8]{0:T(128)S(1)} %dynamic-update-slice.3, f32[8]{0:T(128)S(1)} %dynamic-update-slice.7), channel_id=1, replica_groups=mesh['tm_0'=4,'tm_1'=2,'src_0'=8,'src_1'=8] {'src_1'}, use_global_device_ids=true, to_apply=%add.3 | all-reduce | flops 16 | bytes 128
  (136 shorter events, 42.4 us)
Async XLA Ops:
  57.4 40.4 %all-to-all-start = ((f32[64,272,8]{1,2,0:T(8,128)}), f32[64,272,8]{1,2,0:T(8,128)S(1)}, u32[]{:S(2)}, u32[]{:S(2)}) async-start(f32[64,272,8]{1,2,0:T(8,128)} %bitcast.2), calls=%async_computation | async-start | bytes 1572864 | tf_op jit(solution)/shard_map/all_to_all | solution.py:20
  74.0 28.0 %copy-start.1 = (f32[8]{0:T(128)S(1)}, f32[8]{0:T(128)}, u32[]{:S(2)}) copy-start(f32[8]{0:T(128)} %param.13) | copy-start | bytes 100
  114.8 74.6 %copy-start = (f32[16,8]{0,1:T(8,128)}, f32[16,8]{0,1:T(8,128)S(1)}, u32[]{:S(2)}) copy-start(f32[16,8]{0,1:T(8,128)S(1)} %stack.67) | copy-start | bytes 1540
